TPU v7x, 512 devices: a 8x2x16 block of a 8x8x16 slice. The times are simulated.
512 devices in a mesh: grp: 2 (over y), dp: 256 (over z, x, core).
Axes of the slice: x: 8, y: 2, z: 16, core: 2. Of those that a mesh axis runs over, the one named last changes fastest.
The devices are a block of a 8x8x16 slice.
Arguments:
- params: float32 [1900544], P(('grp', 'dp')), parts along dimension 0, may hold values from -0.3 to 0.3
- momentum: float32 [1900544], P(('grp', 'dp')), parts along dimension 0, may hold values from -6 to 6
- noise_draws: float32 [2, 950272], P('grp', 'dp'), parts along dimension 0, may hold values from -6 to 6
- images: float32 [262144, 448], P(('grp', 'dp')), parts along dimension 0, may hold values from -6 to 6
- labels: int32 [262144], P(('grp', 'dp')), parts along dimension 0, may hold values from 0 to 9
- indices: int32 [2, 65536], P('grp', 'dp'), parts along dimension 0, may hold values from 0 to 511
Outputs:
- params_out: float32 [1900544], P(('grp', 'dp')), parts along dimension 0
- momentum_out: float32 [1900544], P(('grp', 'dp')), parts along dimension 0
- losses: float32 [2], P('grp'), parts along dimension 0
There are 2 independent parts, one for each index of `grp`. A program takes and returns all parts, laid end to end along the dimension named above; each array names one. Nothing has to cross between parts.
All inputs are finite; a program needn't handle non-finite values.
Results may differ from a plain program's by a relative error of at most 0.0003.
Values sent between devices are 32-bit elements; how exact they have to be, the bound alone decides.
A program may use at most 64 MiB of HBM per device.

v0:
```python
import math
import jax
import jax.numpy as jnp
from jax import lax
from jax.sharding import Mesh
from jax.sharding import PartitionSpec as P

DIN = 448
H = 2048
OUT = 10
DP = ("dp_0", "dp_1", "dp_2")
GRP_DP = ("grp", "dp_0", "dp_1", "dp_2")
step_size = 0.02
friction = 15.0


def laid_out(parts, dim):
    dims = list(parts.shape[1:])
    dims[dim] *= parts.shape[0]
    return jnp.moveaxis(parts, 0, dim).reshape(dims)


def gather_in_order(value, axes, turns):
    parts = value[None]
    for k in turns:
        parts = lax.all_gather(parts, axes[k], axis=0, tiled=True)
    block = [lax.axis_size(axes[k]) for k in reversed(turns)]
    parts = parts.reshape(*block, *value.shape)
    turned = sorted(range(len(turns)), key=lambda place: turns[len(turns) - 1 - place])
    return parts.transpose(*turned, *range(len(turns), parts.ndim)).reshape(-1, *value.shape)


def gathered_by_axis(value, axes, turns, dim):
    return laid_out(gather_in_order(value, axes, turns), dim)


def one_axis_at_a_time(value, axes):
    for axis in axes:
        value = lax.psum(value, axis)
    return value


def own_block(parts, axes, turns):
    dims = [lax.axis_size(a) for a in axes]
    parts = parts.reshape(*dims, *parts.shape[1:])
    parts = parts.transpose(*turns, *range(len(axes), parts.ndim))
    parts = parts.reshape(-1, *parts.shape[len(axes) :])
    for k in turns:
        parts = lax.psum_scatter(parts, axes[k], scatter_dimension=0, tiled=True)
    return parts[0]


def cut_along(value, dim, size):
    before, after = (value.shape[:dim], value.shape[dim + 1 :])
    return jnp.moveaxis(value.reshape(*before, size, -1, *after), dim, 0)


def scatter_axes(value, axes, turns, dim):
    size = lax.axis_size(axes)
    return own_block(cut_along(value, dim, size), axes, turns)


def unpack(flat_vec):
    in_end = DIN * H
    w_in = flat_vec[:in_end].reshape(DIN, H)
    b_in = flat_vec[in_end : in_end + H]
    hid_end = in_end + H
    w_out = flat_vec[hid_end : hid_end + H * OUT].reshape(H, OUT)
    b_out = flat_vec[hid_end + H * OUT : hid_end + H * OUT + OUT]
    return (w_in, b_in, w_out, b_out)


def total_nll(flat_vec, chosen_rows, targets):
    w_in, b_in, w_out, b_out = unpack(flat_vec)
    hidden = jnp.tanh(
        jnp.dot(
            chosen_rows, w_in, precision=lax.Precision.HIGHEST, preferred_element_type=jnp.float32
        )
        + b_in
    )
    logits = (
        jnp.dot(hidden, w_out, precision=lax.Precision.HIGHEST, preferred_element_type=jnp.float32)
        + b_out
    )
    log_norm = jnp.log(jnp.sum(jnp.exp(logits), axis=1))
    classes = lax.broadcasted_iota(jnp.int32, logits.shape, 1)
    picked = jnp.sum(jnp.where(targets[:, None] == classes, logits, 0.0), axis=1)
    return jnp.sum(log_norm - picked)


def prior_precision(flat_index):
    in_end = DIN * H
    hid_end = in_end + H
    out_end = hid_end + H * OUT
    return jnp.where(
        flat_index < in_end,
        float(DIN),
        jnp.where(flat_index < hid_end, 1.0, jnp.where(flat_index < out_end, float(H), 1.0)),
    )


def body(params, momentum, noise_draws, images, labels, indices):
    shard_len = params.shape[0]
    shard_start = lax.axis_index(DP) * shard_len
    precision = prior_precision(shard_start + lax.iota(jnp.int32, shard_len))
    scale_data = images.shape[0] / indices.shape[1]
    row_count = lax.axis_size(DP) * indices.shape[1]
    gathered = gathered_by_axis(params, DP, (0, 1, 2), 0)
    picked_rows = indices[0]
    chosen_rows = jnp.take(images, picked_rows, axis=0)
    targets = jnp.take(labels, picked_rows, axis=0)
    nll_part, pullback = jax.vjp(
        lambda weights_flat: total_nll(weights_flat, chosen_rows, targets), gathered
    )
    (local_grad,) = pullback(jnp.ones_like(nll_part))
    losses = [one_axis_at_a_time(nll_part, DP) / row_count]
    own_grad = scatter_axes(local_grad, DP, (2, 0, 1), 0)
    total_force = scale_data * own_grad + precision * params
    momentum = (
        (1.0 - step_size * friction) * momentum
        - step_size * total_force
        + math.sqrt(2.0 * friction * step_size) * noise_draws[0]
    )
    params = params + step_size * momentum
    return (params, momentum, jnp.stack(losses))


def solution(mesh):
    torus = Mesh(mesh.devices.reshape(mesh.shape["grp"], 16, 8, 2), ("grp", "dp_0", "dp_1", "dp_2"))
    placed = (P(GRP_DP), P(GRP_DP), P("grp", DP), P(GRP_DP, None), P(GRP_DP), P("grp", DP))
    return jax.shard_map(
        body,
        mesh=torus,
        in_specs=placed,
        out_specs=(P(GRP_DP), P(GRP_DP), P("grp")),
        check_vma=False,
    )
```

profile of v0, /device:TPU:66, one launch (start us, length us, event | category | flops | bytes accessed | tf_op | source)
XLA Modules:
  0.0 469.8 jit_solution(17000663822888148046)
XLA Ops:
  8.1 69.3 %all-gather.1 = f32[16,1,3712]{2,1,0:T(1,128)S(1)} all-gather(f32[1,1,3712]{2,1,0:T(1,128)S(1)} %reshape.105), channel_id=2, replica_groups=mesh['grp'=2,'dp_0'=16,'dp_1'=8,'dp_2'=2] {'dp_0'}, dimensions={0}, use_global_device_ids=true | all-gather | bytes 252416 | tf_op jit(solution)/shard_map/all_gather | solution.py:26
  78.3 40.2 %all-gather.5.cloned.1.call-done = f32[128,3712]{1,0:T(8,128)} async-done(((f32[16,3712]{1,0:T(8,128)}), f32[128,3712]{1,0:T(8,128)}) %all-gather.5.cloned.1.call-update) | async-done | bytes 1900560 | tf_op jit(solution)/shard_map/all_gather | solution.py:26
  119.9 1.9 gather_fusion
  121.9 22.7 %all-gather.7.cloned.1.call-done = f32[256,3712]{1,0:T(8,128)} async-done(((f32[128,3712]{1,0:T(8,128)}), f32[256,3712]{1,0:T(8,128)}) %all-gather.7.cloned.1.call-update) | async-done | bytes 3801104 | tf_op jit(solution)/shard_map/all_gather | solution.py:26
  144.6 6.8 %copy.18 = f32[16,8,2,3712]{3,2,1,0:T(2,128)} copy(f32[16,8,2,3712]{3,0,1,2:T(8,128)} %bitcast.26) | data formatting | bytes 7602176 | tf_op jit(solution)/shard_map/transpose | solution.py:30
  151.5 5.8 %slice.15 = f32[464,2048]{1,0:T(8,128)} reshape(f32[16,8,2,3712]{3,2,1,0:T(2,128)} %copy.18) | data formatting | bytes 7602176 | tf_op jit(solution)/shard_map/jvp()/slice | solution.py:65
  157.3 5.9 %reshape_reshape.6 = f32[950272]{0:T(1024)} reshape(f32[16,8,2,3712]{3,2,1,0:T(2,128)} %copy.18) | data formatting | bytes 7602176 | tf_op jit(solution)/shard_map/reshape;reshape | solution.py:20
  165.9 5.7 %fusion.5 = f32[256,2048]{1,0:T(8,128)S(1)} fusion(f32[464,2048]{1,0:T(8,128)} %slice.15, f32[2048]{0:T(1024)S(1)} %slice.25, f32[256,448]{1,0:T(8,128)S(1)} %gather_fusion.1, pred[256]{0:T(512)(128)(4,1)S(1)} %get-tuple-element.8), kind=kOutput, calls=%fused_computation.6 | convolution fusion | flops 2819211264 | bytes 6234368 | tf_op jit(solution)/shard_map/jvp()/dot_general | solution.py:76
  171.6 1.9 exponential_reduce_fusion
  173.5 2.1 fusion.26
  175.6 3.6 fusion.18
  179.4 3.6 convolution_bitcast_fusion
  183.0 2.6 copy.24
  186.4 4.1 pad_add_fusion
  190.5 5.5 %reshape_reshape.7 = f32[16,8,2,3712]{3,2,1,0:T(2,128)} reshape(f32[950272]{0:T(1024)} %pad_add_fusion) | data formatting | bytes 7602176 | tf_op jit(solution)/shard_map/reshape;reshape | solution.py:45
  196.0 4.1 copy.21
  200.3 25.6 %reduce-scatter.2.cloned.1.call-done = f32[128,3712]{1,0:T(8,128)} async-done(((f32[256,3712]{1,0:T(8,128)}), f32[128,3712]{1,0:T(8,128)}) %reduce-scatter.2.cloned.1.call-update) | async-done | bytes 1900560 | tf_op jit(solution)/shard_map/reduce_scatter | solution.py:49
  227.9 148.8 %all-reduce.9.cloned.1.call-done = f32[128,3712]{1,0:T(8,128)} async-done(((f32[128,3712]{1,0:T(8,128)}), f32[128,3712]{1,0:T(8,128)}) %all-reduce.9.cloned.1.call-update) | async-done | bytes 1900560
  376.7 1.6 constant_dynamic-slice_fusion
  380.2 29.9 %psum.21 = f32[]{:T(128)} all-reduce(f32[]{:T(128)} %subtract_reduce_fusion), channel_id=1, replica_groups=mesh['grp'=2,'dp_0'=16,'dp_1'=8,'dp_2'=2] {'dp_0'}, use_global_device_ids=true, to_apply=%region_8.9 | all-reduce | flops 1 | bytes 8 | tf_op jit(solution)/shard_map/psum | solution.py:39
  410.1 16.3 %psum.22 = f32[]{:T(128)} all-reduce(f32[]{:T(128)} %psum.21), channel_id=1, replica_groups=mesh['grp'=2,'dp_0'=16,'dp_1'=8,'dp_2'=2] {'dp_1'}, use_global_device_ids=true, to_apply=%region_9.10 | all-reduce | flops 1 | bytes 8 | tf_op jit(solution)/shard_map/psum | solution.py:39
  426.4 3.1 psum.23
  430.2 29.6 %all-reduce.11.cloned.1.call-done = f32[8,3712]{1,0:T(8,128)} async-done(((f32[8,3712]{1,0:T(8,128)}), f32[8,3712]{1,0:T(8,128)}) %all-reduce.11.cloned.1.call-update) | async-done | bytes 118800
  459.8 1.6 fusion.17
  (42 shorter events, 10.8 us)
Async XLA Ops:
  7.2 112.7 %copy-start = (s32[512]{0:T(512)S(1)}, s32[512]{0:T(512)}, u32[]{:S(2)}) copy-start(s32[512]{0:T(512)} %param.10) | copy-start | bytes 6148
  7.2 111.4 %copy-start.1 = (f32[512,448]{0,1:T(8,128)S(1)}, f32[512,448]{0,1:T(8,128)}, u32[]{:S(2)}) copy-start(f32[512,448]{0,1:T(8,128)} %param.9) | copy-start | bytes 2752516
  7.2 111.2 %all-gather.5.cloned.1.call-start = ((), (), s32[]{:S(2)}) async-start(), calls=%async_computation.1 | async-start | bytes 2138112 | tf_op jit(solution)/shard_map/all_gather | solution.py:26
  78.1 40.8 %copy-start.5 = (s32[1,256]{1,0:T(1,128)S(1)}, s32[1,256]{1,0:T(1,128)}, u32[]{:S(2)}) copy-start(s32[1,256]{1,0:T(1,128)} %param.11) | copy-start | bytes 3076
  78.2 66.5 %all-gather.7.cloned.1.call-start = ((), (), s32[]{:S(2)}) async-start(), calls=%async_computation.2 | async-start | bytes 5701632 | tf_op jit(solution)/shard_map/all_gather | solution.py:26
  118.5 107.4 %reduce-scatter.2.cloned.1.call-start = ((), (), s32[]{:S(2)}) async-start(), calls=%async_computation.3 | async-start | bytes 5701632 | tf_op jit(solution)/shard_map/reduce_scatter | solution.py:49
  165.9 5.7 %slice-start = ((f32[950272]{0:T(1024)}), f32[10]{0:T(128)S(1)}, s32[]{:S(2)}) async-start(f32[950272]{0:T(1024)} %reshape_reshape.6), calls=%async_computation.6 | async-start | bytes 1024 | tf_op jit(solution)/shard_map/jvp()/slice | solution.py:69
  200.2 178.1 %copy-start.4 = (f32[1,3712]{1,0:T(1,128)S(1)}, f32[1,3712]{1,0:T(1,128)}, u32[]{:S(2)}) copy-start(f32[1,3712]{1,0:T(1,128)} %param.8) | copy-start | bytes 44548
  200.2 261.3 %copy-start.2 = (f32[3712]{0:T(1024)S(1)}, f32[3712]{0:T(1024)}, u32[]{:S(2)}) copy-start(f32[3712]{0:T(1024)} %param.6) | copy-start | bytes 44548
  200.2 261.3 %copy-start.3 = (f32[3712]{0:T(1024)S(1)}, f32[3712]{0:T(1024)}, u32[]{:S(2)}) copy-start(f32[3712]{0:T(1024)} %param.7) | copy-start | bytes 44548
  200.2 176.5 %all-reduce.9.cloned.1.call-start = ((), (), s32[]{:S(2)}) async-start(), calls=%async_computation.4 | async-start | bytes 3801088
  225.9 233.9 %all-reduce.11.cloned.1.call-start = ((), (), s32[]{:S(2)}) async-start(), calls=%async_computation.5 | async-start | bytes 237568
Sparse Core Ops, SparseCore 0:
  78.3 40.0 all-gather.4
  120.5 24.0 all-gather.6
  200.3 25.5 reduce-scatter.1
  228.1 148.4 all-reduce.8
  378.9 80.9 all-reduce.10
where the time goes:
time: 470 us
  waiting for transfers between devices  267 us (57%)
  blocking collectives  119 us (25%)
  local copies, waits for them, and re-layouts  43.1 us (9%)
  matrix products  16.9 us (4%)
  between operations  16.5 us (4%)
  other arithmetic  7.13 us (2%)
    unnamed x7, waiting for transfers between devices  179 us
    all_gather x1, blocking collectives, gather_in_order(): parts = lax.all_gather(parts, axes[k], axis=0, tiled=True)  69.3 us
    all_gather x2, waiting for transfers between devices, gather_in_order(): parts = lax.all_gather(parts, axes[k], axis=0, tiled=True)  62.9 us
    psum x3, blocking collectives, one_axis_at_a_time(): value = lax.psum(value, axis)  49.3 us
    reduce_scatter x1, waiting for transfers between devices, own_block(): parts = lax.psum_scatter(parts, axes[k], scatter_dimension=0, tiled=True)  25.6 us
  transfers between devices with their start and end apart: 5, of which 5 were waited for; matrix products, arithmetic and copies ran while one was open for 1% of the time, Pallas kernels for 0%

commit v1 on v0

--- a/solution.py
+++ b/solution.py
@@ -4,6 +4,7 @@
 from jax import lax
 from jax.sharding import Mesh
 from jax.sharding import PartitionSpec as P
+from jax.lax import all_to_all, axis_size
 
 DIN = 448
 H = 2048
@@ -23,7 +24,9 @@
 def gather_in_order(value, axes, turns):
     parts = value[None]
     for k in turns:
-        parts = lax.all_gather(parts, axes[k], axis=0, tiled=True)
+        u_in = axes[k]
+        current_arr = axis_size(u_in)
+        parts = jnp.concatenate(all_to_all(jnp.stack(current_arr * [parts], 0), u_in, 0, 0), 0)
     block = [lax.axis_size(axes[k]) for k in reversed(turns)]
     parts = parts.reshape(*block, *value.shape)
     turned = sorted(range(len(turns)), key=lambda place: turns[len(turns) - 1 - place])

time: 470 us -> 445 us (0.947)
  waiting for transfers between devices: 267 us -> 236 us
  starting transfers between devices: 0.31 us -> 7.97 us
    all_gather x1 -> x0, blocking collectives: 69.3 us -> none  [gather_in_order(): parts = lax.all_gather(parts, axes[k], axis=0, tiled=True)]
    all_to_all x0 -> x2, blocking collectives: none -> 67.7 us  [gather_in_order(): all_to_all(jnp.stack(current_arr * [parts], 0), u_in, 0, 0)]
    all_gather x2 -> x0, waiting for transfers between devices: 62.9 us -> none  [gather_in_order(): parts = lax.all_gather(parts, axes[k], axis=0, tiled=True)]
    all_to_all x0 -> x1, waiting for transfers between devices: none -> 36.5 us  [gather_in_order(): all_to_all(jnp.stack(current_arr * [parts], 0), u_in, 0, 0)]
    all_to_all x0 -> x1, starting transfers between devices: none -> 7.84 us  [gather_in_order(): all_to_all(jnp.stack(current_arr * [parts], 0), u_in, 0, 0)]
    reduce_scatter x1, waiting for transfers between devices: 25.6 us -> 20.1 us  [own_block(): parts = lax.psum_scatter(parts, axes[k], scatter_dimension=0, tiled=True)]
    unnamed x7 -> x5, waiting for transfers between devices: 179 us -> 179 us
  transfers between devices with their start and end apart: 5 -> 4, of which waited for: 5 -> 4; matrix products, arithmetic and copies ran while one was open for 1% -> 2% of each run, Pallas kernels for 0% -> 0%
where the time goes in v1:
time: 445 us; the launch traced here: 444 us
  waiting for transfers between devices  236 us (53%)
  blocking collectives  117 us (26%)
  local copies, waits for them, and re-layouts  43 us (10%)
  matrix products  16.9 us (4%)
  between operations  16.4 us (4%)
  starting transfers between devices  7.97 us (2%)
  other arithmetic  7.38 us (2%)
    unnamed x5, waiting for transfers between devices  179 us
    all_to_all x2, blocking collectives, gather_in_order(): all_to_all(jnp.stack(current_arr * [parts], 0), u_in, 0, 0)  67.7 us
    psum x3, blocking collectives, one_axis_at_a_time(): value = lax.psum(value, axis)  49.3 us
    all_to_all x1, waiting for transfers between devices, gather_in_order(): all_to_all(jnp.stack(current_arr * [parts], 0), u_in, 0, 0)  36.5 us
    reduce_scatter x1, waiting for transfers between devices, own_block(): parts = lax.psum_scatter(parts, axes[k], scatter_dimension=0, tiled=True)  20.1 us
    dot_general x2, matrix products, total_nll(): jnp.dot(chosen_rows, w_in, precision=lax.Precision.HIGHEST, preferred_ele...  9.32 us
  transfers between devices with their start and end apart: 4, of which 4 were waited for; matrix products, arithmetic and copies ran while one was open for 2% of the time, Pallas kernels for 0%

profile of v1, /device:TPU:66, one launch (start us, length us, event | category | flops | bytes accessed | tf_op | source)
XLA Modules:
  0.0 444.4 jit_solution(14905619418884683783)
XLA Ops:
  8.0 60.9 %all_to_all.15 = f32[16,1,3712]{2,1,0:T(1,128)S(1)} all-to-all(f32[16,1,3712]{2,1,0:T(1,128)S(1)} %stack.12), channel_id=1, replica_groups=mesh['grp'=2,'dp_0'=16,'dp_1'=8,'dp_2'=2] {'dp_0'}, dimensions={0} | all-to-all | bytes 475136 | tf_op jit(solution)/shard_map/all_to_all | solution.py:29
  70.3 7.8 %all-to-all-start.1 = ((f32[8,16,3712]{2,1,0:T(8,128)}), f32[8,16,3712]{2,1,0:T(8,128)S(1)}, u32[]{:S(2)}, u32[]{:S(2)}) async-start(f32[8,16,3712]{2,1,0:T(8,128)} %stack.13), calls=%async_computation.1 | async-start | bytes 3801088 | tf_op jit(solution)/shard_map/all_to_all | solution.py:29
  80.7 1.9 gather_fusion
  82.7 36.5 %all-to-all-done.1 = f32[8,16,3712]{2,1,0:T(8,128)S(1)} async-done(((f32[8,16,3712]{2,1,0:T(8,128)}), f32[8,16,3712]{2,1,0:T(8,128)S(1)}, u32[]{:S(2)}, u32[]{:S(2)}) %all-to-all-start.1) | async-done | bytes 1900576 | tf_op jit(solution)/shard_map/all_to_all | solution.py:29
  119.4 6.8 %all_to_all.16 = f32[2,128,3712]{2,1,0:T(8,128)S(1)} all-to-all(f32[2,128,3712]{2,1,0:T(8,128)S(1)} %pad_maximum_fusion), channel_id=1, replica_groups=mesh['grp'=2,'dp_0'=16,'dp_1'=8,'dp_2'=2] {'dp_2'}, dimensions={0} | all-to-all | bytes 7602176 | tf_op jit(solution)/shard_map/all_to_all | solution.py:29
  126.2 4.8 %copy.18 = f32[16,8,2,3712]{3,2,1,0:T(2,128)} copy(f32[16,8,2,3712]{3,0,1,2:T(8,128)S(1)} %bitcast.25) | data formatting | bytes 7602176 | tf_op jit(solution)/shard_map/transpose | solution.py:33
  131.0 5.8 %slice.15 = f32[464,2048]{1,0:T(8,128)} reshape(f32[16,8,2,3712]{3,2,1,0:T(2,128)} %copy.18) | data formatting | bytes 7602176 | tf_op jit(solution)/shard_map/jvp()/slice | solution.py:68
  136.8 5.9 %reshape_reshape.10 = f32[950272]{0:T(1024)} reshape(f32[16,8,2,3712]{3,2,1,0:T(2,128)} %copy.18) | data formatting | bytes 7602176 | tf_op jit(solution)/shard_map/reshape;reshape | solution.py:21
  145.4 5.7 %fusion.5 = f32[256,2048]{1,0:T(8,128)S(1)} fusion(f32[464,2048]{1,0:T(8,128)} %slice.15, f32[2048]{0:T(1024)S(1)} %slice.25, f32[256,448]{1,0:T(8,128)S(1)} %gather_fusion.1, pred[256]{0:T(512)(128)(4,1)S(1)} %get-tuple-element.8), kind=kOutput, calls=%fused_computation.7 | convolution fusion | flops 2819211264 | bytes 6234368 | tf_op jit(solution)/shard_map/jvp()/dot_general | solution.py:79
  151.2 1.9 exponential_reduce_fusion
  153.0 2.1 fusion.26
  155.1 3.6 fusion.18
  158.9 3.6 convolution_bitcast_fusion
  162.5 2.6 copy.24
  165.9 4.1 pad_add_fusion
  170.0 5.5 %reshape_reshape.11 = f32[16,8,2,3712]{3,2,1,0:T(2,128)} reshape(f32[950272]{0:T(1024)} %pad_add_fusion) | data formatting | bytes 7602176 | tf_op jit(solution)/shard_map/reshape;reshape | solution.py:48
  175.5 4.1 copy.21
  179.8 20.1 %reduce-scatter.2.cloned.1.call-done = f32[128,3712]{1,0:T(8,128)} async-done(((f32[256,3712]{1,0:T(8,128)}), f32[128,3712]{1,0:T(8,128)}) %reduce-scatter.2.cloned.1.call-update) | async-done | bytes 1900560 | tf_op jit(solution)/shard_map/reduce_scatter | solution.py:52
  201.9 149.2 %all-reduce.9.cloned.1.call-done = f32[128,3712]{1,0:T(8,128)} async-done(((f32[128,3712]{1,0:T(8,128)}), f32[128,3712]{1,0:T(8,128)}) %all-reduce.9.cloned.1.call-update) | async-done | bytes 1900560
  354.7 29.9 %psum.21 = f32[]{:T(128)} all-reduce(f32[]{:T(128)} %subtract_reduce_fusion), channel_id=1, replica_groups=mesh['grp'=2,'dp_0'=16,'dp_1'=8,'dp_2'=2] {'dp_0'}, use_global_device_ids=true, to_apply=%region_8.9 | all-reduce | flops 1 | bytes 8 | tf_op jit(solution)/shard_map/psum | solution.py:42
  384.6 16.3 %psum.22 = f32[]{:T(128)} all-reduce(f32[]{:T(128)} %psum.21), channel_id=1, replica_groups=mesh['grp'=2,'dp_0'=16,'dp_1'=8,'dp_2'=2] {'dp_1'}, use_global_device_ids=true, to_apply=%region_9.10 | all-reduce | flops 1 | bytes 8 | tf_op jit(solution)/shard_map/psum | solution.py:42
  400.9 3.1 psum.23
  404.6 29.8 %all-reduce.11.cloned.1.call-done = f32[8,3712]{1,0:T(8,128)} async-done(((f32[8,3712]{1,0:T(8,128)}), f32[8,3712]{1,0:T(8,128)}) %all-reduce.11.cloned.1.call-update) | async-done | bytes 118800
  434.4 1.6 fusion.17
  (39 shorter events, 14.3 us)
Async XLA Ops:
  7.2 73.5 %copy-start = (s32[512]{0:T(512)S(1)}, s32[512]{0:T(512)}, u32[]{:S(2)}) copy-start(s32[512]{0:T(512)} %param.10) | copy-start | bytes 6148
  70.3 9.4 %copy-start.4 = (s32[1,256]{1,0:T(1,128)S(1)}, s32[1,256]{1,0:T(1,128)}, u32[]{:S(2)}) copy-start(s32[1,256]{1,0:T(1,128)} %param.11) | copy-start | bytes 3076
  70.3 48.9 %all-to-all-start.1 = ((f32[8,16,3712]{2,1,0:T(8,128)}), f32[8,16,3712]{2,1,0:T(8,128)S(1)}, u32[]{:S(2)}, u32[]{:S(2)}) async-start(f32[8,16,3712]{2,1,0:T(8,128)} %stack.13), calls=%async_computation.1 | async-start | bytes 3801088 | tf_op jit(solution)/shard_map/all_to_all | solution.py:29
  78.2 121.7 %reduce-scatter.2.cloned.1.call-start = ((), (), s32[]{:S(2)}) async-start(), calls=%async_computation.4 | async-start | bytes 5701632 | tf_op jit(solution)/shard_map/reduce_scatter | solution.py:52
  145.4 5.7 %slice-start = ((f32[950272]{0:T(1024)}), f32[10]{0:T(128)S(1)}, s32[]{:S(2)}) async-start(f32[950272]{0:T(1024)} %reshape_reshape.10), calls=%async_computation.7 | async-start | bytes 1024 | tf_op jit(solution)/shard_map/jvp()/slice | solution.py:72
  179.7 173.0 %copy-start.3 = (f32[1,3712]{1,0:T(1,128)S(1)}, f32[1,3712]{1,0:T(1,128)}, u32[]{:S(2)}) copy-start(f32[1,3712]{1,0:T(1,128)} %param.8) | copy-start | bytes 44548
  179.7 256.3 %copy-start.1 = (f32[3712]{0:T(1024)S(1)}, f32[3712]{0:T(1024)}, u32[]{:S(2)}) copy-start(f32[3712]{0:T(1024)} %param.6) | copy-start | bytes 44548
  179.7 256.3 %copy-start.2 = (f32[3712]{0:T(1024)S(1)}, f32[3712]{0:T(1024)}, u32[]{:S(2)}) copy-start(f32[3712]{0:T(1024)} %param.7) | copy-start | bytes 44548
  179.7 171.4 %all-reduce.9.cloned.1.call-start = ((), (), s32[]{:S(2)}) async-start(), calls=%async_computation.5 | async-start | bytes 3801088
  199.9 234.5 %all-reduce.11.cloned.1.call-start = ((), (), s32[]{:S(2)}) async-start(), calls=%async_computation.6 | async-start | bytes 237568
Sparse Core Ops, SparseCore 0:
  179.8 19.9 reduce-scatter.1
  202.3 148.8 all-reduce.8
  353.5 80.9 all-reduce.10
